TPU v7x, 32 devices: a whole 2x2x4 slice. The times are simulated.
32 devices in a mesh: grp: 8 (over y, x, core), inner: 4 (over z).
Axes of the slice: x: 2, y: 2, z: 4, core: 2. Of those that a mesh axis runs over, the one named last changes fastest.
Arguments:
- amplitudes: bfloat16 [16, 8, 12288], P('grp', None, 'inner'), may hold values from -6 to 6
- factors: bfloat16 [16, 2000, 12288], P('grp', 'inner'), may hold values from -0.125 to 0.125
- atom_charges: bfloat16 [16, 64, 12288], P('grp', None, 'inner'), may hold values from -0.0068359375 to 0.0068359375
- eps_occ: float32 [16, 48], P('grp'), may hold values from -1.2 to -0.3
- eps_vir: float32 [16, 256], P('grp'), may hold values from 0.1 to 1.5
- occ_count: int32 [16], P('grp'), may hold values from 24 to 48
- vir_count: int32 [16], P('grp'), may hold values from 128 to 256
- atom_list: int32 [1024], P('grp'), may hold values from 0 to 1023, each once
- positions: float32 [3, 1024], replicated, may hold values from 0 to 12
Outputs:
- refined: float32 [16, 8, 12288], P('grp', None, 'inner')
- hamiltonian: float32 [128, 8, 16], P('grp', None, 'inner')
Inputs may be any that keep to these rules, and one draw needn't show every extreme that they name: `atom_list`: every atom index appears exactly once.
All inputs are finite; a program needn't handle non-finite values.
Results may differ from a plain program's by a relative error of at most 0.022.
Values may be sent and summed in bfloat16 or wider, within the bound.
No kernel may reach another device: no remote copies, remote signals or barrier semaphores. Data moves between devices by JAX's collectives and lax.ppermute only.
A program may use at most 64 MiB of HBM per device.

v0:
```python
import jax
import jax.numpy as jnp
from jax import lax
from jax.sharding import PartitionSpec as P

NVIR = 256
STATES = 8
epsilon = 1e-06


def coupling_block(
    group_charges, own_xyz, own_ids, energies, in_charges, in_xyz, slice_rows, inner_pos, monomers
):
    count = in_charges.shape[0]
    offset = own_xyz[:, :, :, None, None] - jnp.transpose(in_xyz, (1, 0, 2))[None, :, None, :, :]
    kernel = 1.0 / jnp.sqrt(jnp.sum(offset * offset, axis=1) + 1.0)
    block = jnp.einsum(
        "csa,carb,rb->csr", group_charges, kernel, in_charges, precision=lax.Precision.HIGHEST
    )
    column = jnp.arange(count, dtype=jnp.int32)
    source = column // slice_rows
    within = inner_pos * slice_rows + column % slice_rows
    in_ids = source * monomers + within // STATES
    in_state = within % STATES
    same = own_ids[:, None, None] == in_ids[None, None, :]
    diag = jnp.arange(STATES, dtype=jnp.int32)[None, :, None] == in_state[None, None, :]
    block = jnp.where(same, jnp.where(diag, energies[:, :, None], 0.0), block)
    return block.reshape(monomers * STATES, count)


def local(
    amplitudes, factors, atom_charges, eps_occ, eps_vir, occ_count, vir_count, atom_list, positions
):
    monomers, states_here, local_pairs = amplitudes.shape
    atom_count = atom_charges.shape[1]
    inner_count = lax.axis_size("inner")
    inner_pos = lax.axis_index("inner")
    pair_index = inner_pos * local_pairs + jnp.arange(local_pairs, dtype=jnp.int32)
    occ_of = pair_index // NVIR
    vir_of = pair_index % NVIR
    active = (
        (occ_of[None, :] < occ_count[:, None]) & (vir_of[None, :] < vir_count[:, None])
    ).astype(jnp.float32)
    gap = jnp.take(eps_vir, vir_of, axis=1) - jnp.take(eps_occ, occ_of, axis=1)
    masked = amplitudes * active[:, None, :].astype(jnp.bfloat16)
    fitted = jnp.einsum(
        "cso,cqo->csq",
        lax.all_gather(masked, "inner", axis=2, tiled=True),
        factors,
        preferred_element_type=jnp.float32,
    )
    fitted_low = fitted.astype(jnp.bfloat16)
    current = masked.astype(jnp.float32)
    partial_value = (
        2.0 * jnp.einsum("csq,cqo->cso", fitted_low, factors, preferred_element_type=jnp.float32)
    ).astype(jnp.bfloat16)
    coulomb = lax.psum_scatter(partial_value, "inner", scatter_dimension=2, tiled=True).astype(
        jnp.float32
    )
    image = gap[:, None, :] * current + coulomb * active[:, None, :]
    numerator, squares = lax.psum(
        (jnp.sum(current * image, axis=2), jnp.sum(current * current, axis=2)), "inner"
    )
    energies = numerator / (squares + epsilon)
    refined = active[:, None, :] * (
        current - (image - energies[:, :, None] * current) / gap[:, None, :]
    )
    refined_low = refined.astype(jnp.bfloat16)
    partial_charges = jnp.einsum(
        "cso,cao->csa", refined_low, atom_charges, preferred_element_type=jnp.float32
    ).reshape(monomers * states_here, atom_count)
    slice_rows = monomers * states_here // inner_count
    group_charges = lax.psum(partial_charges, "inner")
    slice_charges = lax.dynamic_slice_in_dim(group_charges, inner_pos * slice_rows, slice_rows, 0)
    group_charges = group_charges.reshape(monomers, states_here, atom_count)
    own_xyz = (
        jnp.take(positions, atom_list, axis=1).reshape(3, monomers, atom_count).transpose(1, 0, 2)
    )
    slice_index = inner_pos * slice_rows + jnp.arange(slice_rows, dtype=jnp.int32)
    slice_xyz = jnp.take(own_xyz, slice_index // STATES, axis=0)
    group_pos = lax.axis_index("grp")
    groups = lax.axis_size("grp")
    own_ids = group_pos * monomers + jnp.arange(monomers, dtype=jnp.int32)
    block = coupling_block(
        group_charges,
        own_xyz,
        own_ids,
        energies,
        lax.all_gather(slice_charges, "grp", axis=0, tiled=True),
        lax.all_gather(slice_xyz, "grp", axis=0, tiled=True),
        slice_rows,
        inner_pos,
        monomers,
    )
    return (refined, block.reshape(monomers * states_here, groups, slice_rows))


def solution(mesh):
    in_specs = (
        P("grp", None, "inner"),
        P("grp", "inner", None),
        P("grp", None, "inner"),
        P("grp", None),
        P("grp", None),
        P("grp"),
        P("grp"),
        P("grp"),
        P(),
    )
    out_specs = (P("grp", None, "inner"), P("grp", None, "inner"))
    return jax.shard_map(local, mesh=mesh, in_specs=in_specs, out_specs=out_specs, check_vma=False)
```

profile of v0, /device:TPU:0, one launch (start us, length us, event | category | flops | bytes accessed | tf_op | source)
XLA Modules:
  0.0 175.4 jit_solution(12270682259931202777)
XLA Ops:
  7.3 0.8 fusion.36
  8.1 0.9 broadcast_multiply_fusion
  9.0 16.3 %all_gather.9 = bf16[2,8,12288]{2,1,0:T(8,128)(2,1)S(1)} all-gather(bf16[2,8,3072]{2,1,0:T(8,128)(2,1)S(1)} %broadcast_multiply_fusion), channel_id=1, replica_groups=mesh['grp'=8,'inner'=4] {'inner'}, dimensions={2}, use_global_device_ids=true | all-gather | bytes 491520 | tf_op jit(solution)/shard_map/all_gather | solution.py:48
  25.3 64.8 %fusion.7 = bf16[2,8,12288]{2,1,0:T(8,128)(2,1)} fusion(bf16[2,500,12288]{2,0,1:T(2,128)(2,1)} %param.10, bf16[2,8,12288]{2,1,0:T(8,128)(2,1)S(1)} %all_gather.9), kind=kOutput, calls=%fused_computation.9 | convolution fusion | flops 393617216 | bytes 25362432 | tf_op jit(solution)/shard_map/csq,cqo->cso/dot_general | solution.py:55
  90.1 0.1 compare_select_fusion
  90.3 0.1 copy.45
  90.5 0.1 copy.46
  90.6 10.8 %gather_fusion = f32[3072,2]{1,0:T(8,128)} fusion(f32[2,256]{0,1:T(8,128)S(1)} %copy.45, s32[3072]{0:T(1024)S(1)} %broadcast_clamp_fusion.1), kind=kCustom, calls=%fused_computation | custom fusion | bytes 61440 | tf_op jit(solution)/shard_map/jit(_take)/gather | solution.py:44
  101.4 10.8 %gather_fusion.1 = f32[3072,2]{1,0:T(8,128)} fusion(f32[2,48]{0,1:T(8,128)S(1)} %copy.46, s32[3072]{0:T(1024)S(1)} %broadcast_clamp_fusion), kind=kCustom, calls=%fused_computation.1 | custom fusion | bytes 61440 | tf_op jit(solution)/shard_map/jit(_take)/gather | solution.py:44
  112.2 3.8 %subtract_bitcast_fusion = f32[2,3072]{0,1:T(8,128)S(1)} fusion(f32[3072,2]{1,0:T(8,128)} %gather_fusion.1, f32[3072,2]{1,0:T(8,128)} %gather_fusion, pred[3072]{0:T(1024)(128)(4,1)S(1)} %get-tuple-element.14, pred[3072]{0:T(1024)(128)(4,1)S(1)} %get-tuple-element.15), kind=kLoop, calls=%fused_computation.14 | loop fusion | flops 18432 | bytes 79872 | tf_op jit(solution)/shard_map/sub | solution.py:44
  116.0 0.5 copy.47
  116.5 0.2 copy.50
  116.7 0.6 gather_fusion.2
  117.4 0.1 copy.51
  117.4 0.1 broadcast_in_dim.94
  117.6 0.6 gather_fusion.3
  118.1 0.1 broadcast_select_fusion
  118.2 9.2 %all_gather.10 = f32[32,3,64]{2,1,0:T(4,128)S(1)} all-gather(f32[4,3,64]{2,1,0:T(4,128)S(1)} %broadcast_select_fusion), channel_id=1, replica_groups=mesh['grp'=8,'inner'=4] {'grp'}, dimensions={0}, use_global_device_ids=true | all-gather | bytes 27648 | tf_op jit(solution)/shard_map/all_gather | solution.py:90
  127.5 0.1 broadcast_compare_fusion
  127.5 1.1 multiply_reduce_fusion
  128.7 0.3 add_rsqrt_fusion
  129.0 0.6 copy-done.1
  129.6 1.1 fusion.19
  130.6 12.4 %all-reduce = (f32[2,8]{1,0:T(2,128)S(1)}, f32[2,8]{1,0:T(2,128)S(1)}) all-reduce(f32[2,8]{1,0:T(2,128)S(1)} %get-tuple-element.5, f32[2,8]{1,0:T(2,128)S(1)} %get-tuple-element.4), channel_id=1, replica_groups=mesh['grp'=8,'inner'=4] {'inner'}, use_global_device_ids=true, to_apply=%region_2.3 | all-reduce | flops 32 | bytes 256 | tf_op jit(solution)/shard_map/psum | solution.py:61
  143.1 1.0 fusion.22
  144.1 0.3 convolution_bitcast_fusion
  144.4 8.5 %psum.23 = f32[16,64]{1,0:T(8,128)S(1)} all-reduce(f32[16,64]{1,0:T(8,128)S(1)} %convolution_bitcast_fusion), channel_id=1, replica_groups=mesh['grp'=8,'inner'=4] {'inner'}, use_global_device_ids=true, to_apply=%region_5.6 | all-reduce | flops 1024 | bytes 8192 | tf_op jit(solution)/shard_map/psum | solution.py:73
  152.9 8.9 %all-gather = f32[8,4,64]{2,1,0:T(4,128)S(1)} all-gather(f32[1,4,64]{2,1,0:T(4,128)S(1)} %dynamic-slice_bitcast_fusion), channel_id=1, replica_groups=mesh['grp'=8,'inner'=4] {'grp'}, dimensions={0}, use_global_device_ids=true | all-gather | bytes 9216 | tf_op jit(solution)/shard_map/all_gather | solution.py:89
  161.8 5.8 %fusion.10 = f32[32,1,2,64]{3,1,2,0:T(1,128)S(1)} fusion(f32[32,64,1,1]{1,2,3,0:T(1,128)S(1)} %bitcast.34, f32[2,64,32,64]{3,2,1,0:T(8,128)S(1)} %add_rsqrt_fusion), kind=kOutput, calls=%fused_computation.11 | convolution fusion | flops 3145728 | bytes 1073152 | tf_op jit(solution)/shard_map/csa,carb,rb->csr/dot_general | solution.py:17
  167.6 0.2 convolution_select_fusion
  167.8 0.1 copy.53
  167.9 0.7 reshape_reshape.3
  (33 shorter events, 0.3 us)
Async XLA Ops:
  7.2 136.9 %copy-start = (bf16[2,64,3072]{2,1,0:T(8,128)(2,1)S(1)}, bf16[2,64,3072]{2,1,0:T(8,128)(2,1)}, u32[]{:S(2)}) copy-start(bf16[2,64,3072]{2,1,0:T(8,128)(2,1)} %param.11) | copy-start | bytes 2359300
  7.2 121.8 %reduce-scatter.2.cloned.1.call-start = ((), (), s32[]{:S(2)}) async-start(), calls=%async_computation.1 | async-start | bytes 491520 | tf_op jit(solution)/shard_map/reduce_scatter | solution.py:57
  25.3 65.0 %copy-start.6 = (s32[128]{0:T(128)S(1)}, s32[128]{0:T(128)}, u32[]{:S(2)}) copy-start(s32[128]{0:T(128)} %param.16) | copy-start | bytes 1540
  25.3 65.1 %copy-start.4 = (f32[2,256]{1,0:T(2,128)S(1)}, f32[2,256]{1,0:T(2,128)}, u32[]{:S(2)}) copy-start(f32[2,256]{1,0:T(2,128)} %param.13) | copy-start | bytes 6148
  25.3 65.2 %copy-start.5 = (f32[2,48]{1,0:T(2,128)S(1)}, f32[2,48]{1,0:T(2,128)}, u32[]{:S(2)}) copy-start(f32[2,48]{1,0:T(2,128)} %param.12) | copy-start | bytes 1156
  112.2 4.3 %copy-start.3 = (f32[3,1024]{1,0:T(4,128)S(1)}, f32[3,1024]{1,0:T(4,128)}, u32[]{:S(2)}) copy-start(f32[3,1024]{1,0:T(4,128)} %param.17) | copy-start | bytes 36868
  128.7 0.9 copy-start.1
  144.1 24.5 %copy-start.2 = (f32[2,8,3072]{2,1,0:T(8,128)}, f32[2,8,3072]{2,1,0:T(8,128)S(1)}, u32[]{:S(2)}) copy-start(f32[2,8,3072]{2,1,0:T(8,128)S(1)} %fusion.22) | copy-start | bytes 589828
Sparse Core Ops, SparseCore 0:
  90.2 22.4 reduce-scatter.1
where the time goes:
time: 176 us; the launch traced here: 175 us
  matrix products  71 us (40%)
  blocking collectives  55.3 us (31%)
  local copies, waits for them, and re-layouts  25.3 us (14%)
  between operations  14.3 us (8%)
  other arithmetic  9.37 us (5%)
    dot_general x1, matrix products, local(): jnp.einsum('csq,cqo->cso', fitted_low, factors, preferred_element_type=jn...  64.8 us
    gather x2, local copies, waits for them, and re-layouts, local(): gap = jnp.take(eps_vir, vir_of, axis=1) - jnp.take(eps_occ, occ_of, axis=1)  21.6 us
    all_gather x1, blocking collectives, local(): lax.all_gather(masked, 'inner', axis=2, tiled=True)  16.3 us
    psum x1, blocking collectives, local(): lax.psum((jnp.sum(current * image, axis=2), jnp.sum(current * current, ax...  12.4 us
    all_gather x1, blocking collectives, local(): lax.all_gather(slice_xyz, 'grp', axis=0, tiled=True)  9.24 us
    all_gather x1, blocking collectives, local(): lax.all_gather(slice_charges, 'grp', axis=0, tiled=True)  8.9 us
    psum x1, blocking collectives, local(): group_charges = lax.psum(partial_charges, 'inner')  8.5 us
    dot_general x2, matrix products, coupling_block(): jnp.einsum('csa,carb,rb->csr', group_charges, kernel, in_charges, precisi...  5.94 us
  transfers between devices with their start and end apart: 1, of which 0 were waited for; matrix products, arithmetic and copies ran while one was open for 17% of the time, Pallas kernels for 0%

commit v1 on v0

--- a/solution.py
+++ b/solution.py
@@ -43,12 +43,24 @@
     ).astype(jnp.float32)
     gap = jnp.take(eps_vir, vir_of, axis=1) - jnp.take(eps_occ, occ_of, axis=1)
     masked = amplitudes * active[:, None, :].astype(jnp.bfloat16)
+    size, place = (lax.axis_size("inner"), lax.axis_index("inner"))
+    left = [(i, (i - 1) % size) for i in range(size)]
+    rows = masked.shape[2]
+    held = masked
     fitted = jnp.einsum(
         "cso,cqo->csq",
-        lax.all_gather(masked, "inner", axis=2, tiled=True),
-        factors,
+        held,
+        lax.dynamic_slice_in_dim(factors, place * rows, held.shape[2], axis=2),
         preferred_element_type=jnp.float32,
     )
+    for step in range(1, size):
+        held = lax.ppermute(held, "inner", left)
+        fitted = fitted + jnp.einsum(
+            "cso,cqo->csq",
+            held,
+            lax.dynamic_slice_in_dim(factors, (place + step) % size * rows, held.shape[2], axis=2),
+            preferred_element_type=jnp.float32,
+        )
     fitted_low = fitted.astype(jnp.bfloat16)
     current = masked.astype(jnp.float32)
     partial_value = (

time: 176 us -> 162 us (0.920)
  matrix products: 71 us -> 33 us
  local copies, waits for them, and re-layouts: 25.3 us -> 49.1 us
  blocking collectives: 55.3 us -> 37.3 us
  waiting for transfers between devices: 0.04 us -> 9.64 us
  starting transfers between devices: 0.04 us -> 7.63 us
    dot_general x1, matrix products: 64.8 us -> 13.4 us  [local(): jnp.einsum('csq,cqo->cso', fitted_low, factors, preferred_element_type=jn...]
    unnamed x18 -> x17, local copies, waits for them, and re-layouts: 1.06 us -> 24.7 us
    all_gather x1 -> x0, blocking collectives: 16.3 us -> none  [local(): lax.all_gather(masked, 'inner', axis=2, tiled=True)]
    dot_general x0 -> x3, matrix products: none -> 13.4 us  [the longest x2 8.9 us: local(): jnp.einsum('cso,cqo->csq', held, lax.dynamic_slice_in_dim(factors, (place...]
    reduce_scatter x1, waiting for transfers between devices: 0.02 us -> 9.61 us  [local(): lax.psum_scatter(partial_value, 'inner', scatter_dimension=2, tiled=True)]
    ppermute x0 -> x3, starting transfers between devices: none -> 7.59 us  [local(): held = lax.ppermute(held, 'inner', left)]
    psum x1, blocking collectives: 12.4 us -> 8.52 us  [local(): lax.psum((jnp.sum(current * image, axis=2), jnp.sum(current * current, ax...]
    psum x1, blocking collectives: 8.5 us -> 10.3 us  [local(): group_charges = lax.psum(partial_charges, 'inner')]
  transfers between devices with their start and end apart: 1 -> 4, of which waited for: 0 -> 1; matrix products, arithmetic and copies ran while one was open for 17% -> 42% of each run, Pallas kernels for 0% -> 0%
where the time goes in v1:
time: 162 us; the launch traced here: 161 us
  local copies, waits for them, and re-layouts  49.1 us (30%)
  blocking collectives  37.3 us (23%)
  matrix products  33 us (20%)
  between operations  14.2 us (9%)
  other arithmetic  10.7 us (7%)
  waiting for transfers between devices  9.64 us (6%)
  starting transfers between devices  7.63 us (5%)
    unnamed x17, local copies, waits for them, and re-layouts  24.7 us
    gather x2, local copies, waits for them, and re-layouts, local(): gap = jnp.take(eps_vir, vir_of, axis=1) - jnp.take(eps_occ, occ_of, axis=1)  21.7 us
    dot_general x1, matrix products, local(): jnp.einsum('csq,cqo->cso', fitted_low, factors, preferred_element_type=jn...  13.4 us
    psum x1, blocking collectives, local(): group_charges = lax.psum(partial_charges, 'inner')  10.3 us
    reduce_scatter x1, waiting for transfers between devices, local(): lax.psum_scatter(partial_value, 'inner', scatter_dimension=2, tiled=True)  9.61 us
    all_gather x1, blocking collectives, local(): lax.all_gather(slice_xyz, 'grp', axis=0, tiled=True)  9.39 us
    all_gather x1, blocking collectives, local(): lax.all_gather(slice_charges, 'grp', axis=0, tiled=True)  9.05 us
    dot_general x2, matrix products, local(): jnp.einsum('cso,cqo->csq', held, lax.dynamic_slice_in_dim(factors, (place...  8.9 us
  transfers between devices with their start and end apart: 4, of which 1 were waited for; matrix products, arithmetic and copies ran while one was open for 42% of the time, Pallas kernels for 0%

profile of v1, /device:TPU:0, one launch (start us, length us, event | category | flops | bytes accessed | tf_op | source)
XLA Modules:
  0.0 161.5 jit_solution(7922822152425925926)
XLA Ops:
  7.3 0.8 fusion.49
  8.1 0.9 broadcast_multiply_fusion
  9.0 5.1 %collective-permute-start = (bf16[2,8,3072]{2,1,0:T(8,128)(2,1)S(1)}, bf16[2,8,3072]{2,1,0:T(8,128)(2,1)S(1)}, u32[]{:S(2)}, u32[]{:S(2)}) collective-permute-start(bf16[2,8,3072]{2,1,0:T(8,128)(2,1)S(1)} %broadcast_multiply_fusion), channel_id=1, source_target_pairs={{0,3},{1,0},{2,1},{3,2},{4,7},{5,4},{6,5},{7,6},{8,11},{9,8},{10,9... | collective-permute-start | bytes 294920 | tf_op jit(solution)/shard_map/ppermute | solution.py:57
  14.3 0.7 compare_select_fusion.9
  15.0 0.7 compare_and_fusion.3
  15.7 24.2 %copy.54 = bf16[2,500,12288]{2,1,0:T(8,128)(2,1)} copy(bf16[2,500,12288]{2,0,1:T(2,128)(2,1)} %param.10) | data formatting | bytes 49152000 | tf_op args[1]
  40.1 10.8 %gather_fusion = f32[3072,2]{1,0:T(8,128)} fusion(f32[2,256]{0,1:T(8,128)S(1)} %copy.51, s32[3072]{0:T(1024)S(1)} %broadcast_clamp_fusion.1), kind=kCustom, calls=%fused_computation | custom fusion | bytes 61440 | tf_op jit(solution)/shard_map/jit(_take)/gather | solution.py:44
  51.0 10.8 %gather_fusion.1 = f32[3072,2]{1,0:T(8,128)} fusion(f32[2,48]{0,1:T(8,128)S(1)} %copy.52, s32[3072]{0:T(1024)S(1)} %broadcast_clamp_fusion), kind=kCustom, calls=%fused_computation.1 | custom fusion | bytes 61440 | tf_op jit(solution)/shard_map/jit(_take)/gather | solution.py:44
  61.8 3.7 %subtract_bitcast_fusion = f32[2,3072]{0,1:T(8,128)S(1)} fusion(f32[3072,2]{1,0:T(8,128)} %gather_fusion.1, f32[3072,2]{1,0:T(8,128)} %gather_fusion, pred[3072]{0:T(1024)(128)(4,1)S(1)} %get-tuple-element.14, pred[3072]{0:T(1024)(128)(4,1)S(1)} %get-tuple-element.15), kind=kLoop, calls=%fused_computation.18 | loop fusion | flops 18432 | bytes 79872 | tf_op jit(solution)/shard_map/sub | solution.py:44
  65.6 0.5 copy.53
  66.1 0.2 copy.59
  66.3 0.6 gather_fusion.2
  67.1 4.5 %fusion.7 = f32[2,8,500]{2,1,0:T(8,128)S(1)} fusion(bf16[2,8,3072]{2,1,0:T(8,128)(2,1)S(1)} %broadcast_multiply_fusion, bf16[2,500,12288]{2,1,0:T(8,128)(2,1)} %copy.54, s32[]{:T(128)S(6)} %select_n.217), kind=kOutput, calls=%fused_computation.13 | convolution fusion | flops 49152000 | bytes 6323460 | tf_op jit(solution)/shard_map/cso,cqo->csq/dot_general | solution.py:50
  71.6 0.6 gather_fusion.3
  72.3 0.5 collective-permute-start.1
  72.8 4.5 %fusion.11 = f32[2,8,500]{2,1,0:T(8,128)S(1)} fusion(f32[2,8,500]{2,1,0:T(8,128)S(1)} %fusion.7, bf16[2,8,3072]{2,1,0:T(8,128)(2,1)S(1)} %collective-permute-done, bf16[2,500,12288]{2,1,0:T(8,128)(2,1)} %copy.54, s32[]{:T(128)S(6)} %select_n.219), kind=kOutput, calls=%fused_computation.19 | convolution fusion | flops 49160000 | bytes 6355460 | tf_op jit(solution)/shard_map/cso,cqo->csq/dot_general | solution.py:58
  77.2 2.0 %collective-permute-start.2 = (bf16[2,8,3072]{2,1,0:T(8,128)(2,1)S(1)}, bf16[2,8,3072]{2,1,0:T(8,128)(2,1)S(1)}, u32[]{:S(2)}, u32[]{:S(2)}) collective-permute-start(bf16[2,8,3072]{2,1,0:T(8,128)(2,1)S(1)} %collective-permute-done.1), channel_id=1, source_target_pairs={{0,3},{1,0},{2,1},{3,2},{4,7},{5,4},{6,5},{7,6},{8,11},{9,8},{10,9... | collective-permute-start | bytes 294920 | tf_op jit(solution)/shard_map/ppermute | solution.py:57
  79.2 4.5 %fusion.14 = f32[2,8,500]{2,1,0:T(8,128)S(1)} fusion(f32[2,8,500]{2,1,0:T(8,128)S(1)} %fusion.11, bf16[2,8,3072]{2,1,0:T(8,128)(2,1)S(1)} %collective-permute-done.1, bf16[2,500,12288]{2,1,0:T(8,128)(2,1)} %copy.54, s32[]{:T(128)S(6)} %select_n.221), kind=kOutput, calls=%fused_computation.20 | convolution fusion | flops 49160000 | bytes 6355460 | tf_op jit(solution)/shard_map/cso,cqo->csq/dot_general | solution.py:58
  83.7 13.4 %fusion = bf16[2,8,12288]{2,1,0:T(8,128)(2,1)} fusion(bf16[2,500,12288]{2,1,0:T(8,128)(2,1)} %copy.54, f32[2,8,500]{2,1,0:T(8,128)S(1)} %fusion.14, bf16[2,8,3072]{2,1,0:T(8,128)(2,1)S(1)} %collective-permute-done.2, s32[]{:T(128)S(6)} %select_n.223), kind=kOutput, calls=%fused_computation.5 | convolution fusion | flops 246169216 | bytes 31489284 | tf_op jit(solution)/shard_map/csq,cqo->cso/dot_general | solution.py:67
  97.0 9.4 %all_gather.6 = f32[32,3,64]{2,1,0:T(4,128)S(1)} all-gather(f32[4,3,64]{2,1,0:T(4,128)S(1)} %broadcast_select_fusion), channel_id=1, replica_groups=mesh['grp'=8,'inner'=4] {'grp'}, dimensions={0}, use_global_device_ids=true | all-gather | bytes 27648 | tf_op jit(solution)/shard_map/all_gather | solution.py:102
  106.5 1.1 multiply_reduce_fusion
  107.6 0.3 add_rsqrt_fusion
  107.9 9.6 %reduce-scatter.2.cloned.1.call-done = bf16[2,8,3072]{2,1,0:T(8,128)(2,1)} async-done(((bf16[2,8,12288]{2,1,0:T(8,128)(2,1)}), bf16[2,8,3072]{2,1,0:T(8,128)(2,1)}) %reduce-scatter.2.cloned.1.call-update) | async-done | bytes 98320 | tf_op jit(solution)/shard_map/reduce_scatter | solution.py:69
  117.5 1.1 fusion.27
  118.6 8.5 %all-reduce = (f32[2,8]{1,0:T(2,128)S(1)}, f32[2,8]{1,0:T(2,128)S(1)}) all-reduce(f32[2,8]{1,0:T(2,128)S(1)} %get-tuple-element.5, f32[2,8]{1,0:T(2,128)S(1)} %get-tuple-element.4), channel_id=1, replica_groups=mesh['grp'=8,'inner'=4] {'inner'}, use_global_device_ids=true, to_apply=%region_2.3 | all-reduce | flops 32 | bytes 256 | tf_op jit(solution)/shard_map/psum | solution.py:73
  127.1 1.0 fusion.30
  128.2 0.3 convolution_bitcast_fusion
  128.5 10.3 %psum.23 = f32[16,64]{1,0:T(8,128)S(1)} all-reduce(f32[16,64]{1,0:T(8,128)S(1)} %convolution_bitcast_fusion), channel_id=1, replica_groups=mesh['grp'=8,'inner'=4] {'inner'}, use_global_device_ids=true, to_apply=%region_5.6 | all-reduce | flops 1024 | bytes 8192 | tf_op jit(solution)/shard_map/psum | solution.py:85
  138.8 9.1 %all-gather = f32[8,4,64]{2,1,0:T(4,128)S(1)} all-gather(f32[1,4,64]{2,1,0:T(4,128)S(1)} %dynamic-slice_bitcast_fusion), channel_id=1, replica_groups=mesh['grp'=8,'inner'=4] {'grp'}, dimensions={0}, use_global_device_ids=true | all-gather | bytes 9216 | tf_op jit(solution)/shard_map/all_gather | solution.py:101
  147.9 5.8 %fusion.9 = f32[32,1,2,64]{3,1,2,0:T(1,128)S(1)} fusion(f32[32,64,1,1]{1,2,3,0:T(1,128)S(1)} %bitcast.38, f32[2,64,32,64]{3,2,1,0:T(8,128)S(1)} %add_rsqrt_fusion), kind=kOutput, calls=%fused_computation.15 | convolution fusion | flops 3145728 | bytes 1073152 | tf_op jit(solution)/shard_map/csa,carb,rb->csr/dot_general | solution.py:17
  153.6 0.2 convolution_select_fusion
  153.9 0.7 reshape_reshape.3
  (40 shorter events, 1.0 us)
Async XLA Ops:
  7.2 121.0 %copy-start = (bf16[2,64,3072]{2,1,0:T(8,128)(2,1)S(1)}, bf16[2,64,3072]{2,1,0:T(8,128)(2,1)}, u32[]{:S(2)}) copy-start(bf16[2,64,3072]{2,1,0:T(8,128)(2,1)} %param.11) | copy-start | bytes 2359300
  7.2 110.4 %reduce-scatter.2.cloned.1.call-start = ((), (), s32[]{:S(2)}) async-start(), calls=%async_computation.1 | async-start | bytes 491520 | tf_op jit(solution)/shard_map/reduce_scatter | solution.py:69
  9.0 63.3 %collective-permute-start = (bf16[2,8,3072]{2,1,0:T(8,128)(2,1)S(1)}, bf16[2,8,3072]{2,1,0:T(8,128)(2,1)S(1)}, u32[]{:S(2)}, u32[]{:S(2)}) collective-permute-start(bf16[2,8,3072]{2,1,0:T(8,128)(2,1)S(1)} %broadcast_multiply_fusion), channel_id=1, source_target_pairs={{0,3},{1,0},{2,1},{3,2},{4,7},{5,4},{6,5},{7,6},{8,11},{9,8},{10,9... | collective-permute-start | bytes 294920 | tf_op jit(solution)/shard_map/ppermute | solution.py:57
  15.7 24.2 %copy-start.4 = (f32[2,256]{1,0:T(2,128)S(1)}, f32[2,256]{1,0:T(2,128)}, u32[]{:S(2)}) copy-start(f32[2,256]{1,0:T(2,128)} %param.13) | copy-start | bytes 6148
  15.7 24.4 %copy-start.5 = (f32[2,48]{1,0:T(2,128)S(1)}, f32[2,48]{1,0:T(2,128)}, u32[]{:S(2)}) copy-start(f32[2,48]{1,0:T(2,128)} %param.12) | copy-start | bytes 1156
  39.9 26.2 %copy-start.3 = (f32[3,1024]{1,0:T(4,128)S(1)}, f32[3,1024]{1,0:T(4,128)}, u32[]{:S(2)}) copy-start(f32[3,1024]{1,0:T(4,128)} %param.17) | copy-start | bytes 36868
  72.3 5.0 %collective-permute-start.1 = (bf16[2,8,3072]{2,1,0:T(8,128)(2,1)S(1)}, bf16[2,8,3072]{2,1,0:T(8,128)(2,1)S(1)}, u32[]{:S(2)}, u32[]{:S(2)}) collective-permute-start(bf16[2,8,3072]{2,1,0:T(8,128)(2,1)S(1)} %collective-permute-done), channel_id=1, source_target_pairs={{0,3},{1,0},{2,1},{3,2},{4,7},{5,4},{6,5},{7,6},{8,11},{9,8},{10,9... | collective-permute-start | bytes 294920 | tf_op jit(solution)/shard_map/ppermute | solution.py:57
  77.2 6.4 %collective-permute-start.2 = (bf16[2,8,3072]{2,1,0:T(8,128)(2,1)S(1)}, bf16[2,8,3072]{2,1,0:T(8,128)(2,1)S(1)}, u32[]{:S(2)}, u32[]{:S(2)}) collective-permute-start(bf16[2,8,3072]{2,1,0:T(8,128)(2,1)S(1)} %collective-permute-done.1), channel_id=1, source_target_pairs={{0,3},{1,0},{2,1},{3,2},{4,7},{5,4},{6,5},{7,6},{8,11},{9,8},{10,9... | collective-permute-start | bytes 294920 | tf_op jit(solution)/shard_map/ppermute | solution.py:57
  97.0 20.5 %copy-start.1 = (bf16[2,8,3072]{2,1,0:T(8,128)(2,1)S(1)}, bf16[2,8,3072]{2,1,0:T(8,128)(2,1)}, u32[]{:S(2)}) copy-start(bf16[2,8,3072]{2,1,0:T(8,128)(2,1)} %param.9) | copy-start | bytes 294916
  128.1 26.5 %copy-start.2 = (f32[2,8,3072]{2,1,0:T(8,128)}, f32[2,8,3072]{2,1,0:T(8,128)S(1)}, u32[]{:S(2)}) copy-start(f32[2,8,3072]{2,1,0:T(8,128)S(1)} %fusion.30) | copy-start | bytes 589828
Sparse Core Ops, SparseCore 0:
  97.2 20.3 reduce-scatter.1
